TPU v7x, 32 devices: a whole 2x2x4 slice. The times are simulated.
32 devices in a mesh: dp: 32 (over z, y, x, core), mp: 1.
Axes of the slice: x: 2, y: 2, z: 4, core: 2. Of those that a mesh axis runs over, the one named last changes fastest.
Arguments:
- gradients: bfloat16 [32, 512, 6144], P('dp', None, 'mp'), may hold values from -48 to 48
- weights: bfloat16 [512, 6144], P(None, 'mp'), may hold values from -3 to 3
- master: float32 [512, 6144], P('dp', 'mp'), may hold values from -6 to 6
- moment_one: float32 [512, 6144], P('dp', 'mp'), may hold values from -6 to 6
- moment_two: float32 [512, 6144], P('dp', 'mp'), may hold values from 0.25 to 4
- group_ids: int32 [512], replicated, may hold values from 0 to 15, never falling along the last dimension, each value on 1 to 64 neighbouring positions
Outputs:
- new_weights: bfloat16 [512, 6144], P(None, 'mp')
- new_master: float32 [512, 6144], P('dp', 'mp')
- new_first: float32 [512, 6144], P('dp', 'mp')
- new_second: float32 [512, 6144], P('dp', 'mp')
Inputs may be any that keep to these rules, and one draw needn't show every extreme that they name: `group_ids`: group numbers never fall along the rows; each group has 1 to 64 rows and every group is present.
All inputs are finite; a program needn't handle non-finite values.
Results may differ from a plain program's by a relative error of at most 0.001.
The roundings to bfloat16 on the way count: a program that leaves them out, or rounds other values in their place, can miss the bound.
Values may be sent and summed in bfloat16 or wider, within the bound.
No kernel may reach another device: no remote copies, remote signals or barrier semaphores. Data moves between devices by JAX's collectives and lax.ppermute only.
A program may use at most 64 MiB of HBM per device.

v0:
```python
import jax
import jax.numpy as jnp
from jax import lax
from jax.sharding import PartitionSpec as P

beta_one = 0.9
beta_two = 0.999
adam_eps = 1e-06
weight_decay = 0.01
learn_rate = 0.04
step_count = 100


def on_device(gradients, weights, master, moment_one, moment_two, group_ids):
    owned_rows = master.shape[0]
    rows_all = weights.shape[0]
    groups = rows_all // 32
    replicas = lax.axis_size("dp")
    my_index = lax.axis_index("dp")
    first_own = my_index * owned_rows
    my_groups = lax.dynamic_slice_in_dim(group_ids, first_own, owned_rows, 0)
    member = (my_groups[:, None] == jnp.arange(groups, dtype=jnp.int32)[None, :]).astype(
        jnp.float32
    )
    weight_rows = jnp.dot(jnp.sum(master * master, axis=1), member, precision=lax.Precision.HIGHEST)
    local_grad = gradients[0]
    summed = lax.psum_scatter(local_grad.astype(jnp.float32), "dp", scatter_dimension=0, tiled=True)
    grad_mean = summed / replicas
    new_first = beta_one * moment_one + (1.0 - beta_one) * grad_mean
    new_second = beta_two * moment_two + (1.0 - beta_two) * grad_mean * grad_mean
    correct_one = 1.0 - beta_one**step_count
    correct_two = 1.0 - beta_two**step_count
    update = (
        new_first / correct_one / (jnp.sqrt(new_second / correct_two) + adam_eps)
        + weight_decay * master
    )
    update_rows = jnp.dot(jnp.sum(update * update, axis=1), member, precision=lax.Precision.HIGHEST)
    weight_sq, update_sq = lax.psum((weight_rows, update_rows), ("dp", "mp"))
    trust_ratio = jnp.sqrt(weight_sq / (update_sq + 1e-06))
    row_ratio = jnp.dot(member, trust_ratio, precision=lax.Precision.HIGHEST)
    step_size = learn_rate * row_ratio[:, None] * update
    new_master = master - step_size
    delta_bf = (-step_size).astype(jnp.bfloat16)
    new_weights = (
        weights.astype(jnp.float32)
        + lax.all_gather(delta_bf, "dp", axis=0, tiled=True).astype(jnp.float32)
    ).astype(jnp.bfloat16)
    return (new_weights, new_master, new_first, new_second)


def solution(mesh):
    placed = (P("dp", None, "mp"), P(None, "mp"), P("dp", "mp"), P("dp", "mp"), P("dp", "mp"), P())
    return jax.shard_map(
        on_device,
        mesh=mesh,
        in_specs=placed,
        out_specs=(P(None, "mp"), P("dp", "mp"), P("dp", "mp"), P("dp", "mp")),
        check_vma=False,
    )
```

profile of v0, /device:TPU:0, one launch (start us, length us, event | category | flops | bytes accessed | tf_op | source)
XLA Modules:
  0.0 302.7 jit_solution(6108356624688245434)
XLA Ops:
  7.2 0.0 reduce-scatter.2.cloned.1.call-start
  7.2 9.0 %bitcast_convert_fusion = f32[512,6144]{1,0:T(8,128)} fusion(bf16[1,512,6144]{2,1,0:T(8,128)(2,1)} %param.6), kind=kLoop, calls=%fused_computation.1 | loop fusion | flops 3145728 | bytes 18874368 | tf_op jit(solution)/shard_map/convert_element_type | solution.py:27
  16.2 0.0 copy-start
  16.2 0.0 copy-start.1
  16.2 0.0 copy-start.2
  16.2 0.0 reduce-scatter.2.cloned.1.call-update
  16.2 0.0 all-gather.2.cloned.1.call-start
  16.3 0.8 dynamic_slice.3
  17.1 156.8 %reduce-scatter.2.cloned.1.call-done = f32[16,6144]{1,0:T(8,128)} async-done(((f32[512,6144]{1,0:T(8,128)}), f32[16,6144]{1,0:T(8,128)}) %reduce-scatter.2.cloned.1.call-update) | async-done | bytes 393232 | tf_op jit(solution)/shard_map/reduce_scatter | solution.py:27
  174.0 0.0 copy-done
  174.0 0.0 copy-done.1
  174.0 0.0 copy-done.2
  174.0 2.3 multiply_reduce_fusion
  176.3 0.2 convolution_bitcast_fusion.1
  176.5 0.2 convolution_bitcast_fusion.2
  176.7 39.4 %all-reduce = (f32[16]{0:T(128)S(1)}, f32[16]{0:T(128)S(1)}) all-reduce(f32[16]{0:T(128)S(1)} %convolution_bitcast_fusion.2, f32[16]{0:T(128)S(1)} %convolution_bitcast_fusion.1), channel_id=1, replica_groups=mesh['dp'=32,'mp'=1] {'dp','mp'}, use_global_device_ids=true, to_apply=%region_1.0 | all-reduce | flops 32 | bytes 256 | tf_op jit(solution)/shard_map/psum | solution.py:38
  216.0 0.2 fusion
  216.2 0.9 multiply_subtract_fusion
  217.2 0.0 all-gather.2.cloned.1.call-update
  217.2 68.7 %all-gather.2.cloned.1.call-done = bf16[512,6144]{1,0:T(8,128)(2,1)} async-done(((bf16[16,6144]{1,0:T(8,128)(2,1)}), bf16[512,6144]{1,0:T(8,128)(2,1)}) %all-gather.2.cloned.1.call-update) | async-done | bytes 6291472 | tf_op jit(solution)/shard_map/all_gather | solution.py:46
  285.9 10.0 %add_convert_fusion = bf16[512,6144]{1,0:T(8,128)(2,1)} fusion(bf16[512,6144]{1,0:T(8,128)(2,1)} %all-gather.2.cloned.1.call-done, bf16[512,6144]{1,0:T(8,128)(2,1)} %param.7), kind=kLoop, calls=%fused_computation | loop fusion | flops 12582912 | bytes 18874368 | tf_op jit(solution)/shard_map/convert_element_type | solution.py:47
Async XLA Ops:
  7.2 166.8 %reduce-scatter.2.cloned.1.call-start = ((), (), s32[]{:S(2)}) async-start(), calls=%async_computation.1 | async-start | bytes 12976128 | tf_op jit(solution)/shard_map/reduce_scatter | solution.py:27
  16.2 157.8 %copy-start = (f32[16,6144]{1,0:T(8,128)S(1)}, f32[16,6144]{1,0:T(8,128)}, u32[]{:S(2)}) copy-start(f32[16,6144]{1,0:T(8,128)} %param.8) | copy-start | bytes 1179652
  16.2 157.8 %copy-start.1 = (f32[16,6144]{1,0:T(8,128)S(1)}, f32[16,6144]{1,0:T(8,128)}, u32[]{:S(2)}) copy-start(f32[16,6144]{1,0:T(8,128)} %param.9) | copy-start | bytes 1179652
  16.2 157.8 %copy-start.2 = (f32[16,6144]{1,0:T(8,128)S(1)}, f32[16,6144]{1,0:T(8,128)}, u32[]{:S(2)}) copy-start(f32[16,6144]{1,0:T(8,128)} %param.10) | copy-start | bytes 1179652
  16.2 269.7 %all-gather.2.cloned.1.call-start = ((), (), s32[]{:S(2)}) async-start(), calls=%async_computation.2 | async-start | bytes 6488064 | tf_op jit(solution)/shard_map/all_gather | solution.py:46
Sparse Core Ops, SparseCore 0:
  16.4 157.5 reduce-scatter.1
  217.3 68.5 all-gather.1
where the time goes:
time: 303 us
  waiting for transfers between devices  226 us (75%)
  blocking collectives  39.4 us (13%)
  other arithmetic  22.2 us (7%)
  between operations  14 us (5%)
    reduce_scatter x1, waiting for transfers between devices, on_device(): lax.psum_scatter(local_grad.astype(jnp.float32), 'dp', scatter_dimension=...  157 us
    all_gather x1, waiting for transfers between devices, on_device(): lax.all_gather(delta_bf, 'dp', axis=0, tiled=True).astype(jnp.float32)  68.7 us
    psum x1, blocking collectives, on_device(): weight_sq, update_sq = lax.psum((weight_rows, update_rows), ('dp', 'mp'))  39.4 us
    convert_element_type x1, other arithmetic, on_device(): new_weights = (weights.astype(jnp.float32) + lax.all_gather(delta_bf, 'dp...  9.96 us
    convert_element_type x1, other arithmetic, on_device(): local_grad.astype(jnp.float32)  8.99 us
  transfers between devices with their start and end apart: 2, of which 2 were waited for; matrix products, arithmetic and copies ran while one was open for 0% of the time, Pallas kernels for 0%

commit v1 on v0

--- a/solution.py
+++ b/solution.py
@@ -9,6 +9,11 @@
 weight_decay = 0.01
 learn_rate = 0.04
 step_count = 100
+
+
+def gather_over(block, axis, dim):
+    repeated = jnp.stack([block] * lax.axis_size(axis))
+    return jnp.concatenate(lax.all_to_all(repeated, axis, 0, 0), axis=dim)
 
 
 def on_device(gradients, weights, master, moment_one, moment_two, group_ids):
@@ -42,8 +47,7 @@
     new_master = master - step_size
     delta_bf = (-step_size).astype(jnp.bfloat16)
     new_weights = (
-        weights.astype(jnp.float32)
-        + lax.all_gather(delta_bf, "dp", axis=0, tiled=True).astype(jnp.float32)
+        weights.astype(jnp.float32) + gather_over(delta_bf, "dp", 0).astype(jnp.float32)
     ).astype(jnp.bfloat16)
     return (new_weights, new_master, new_first, new_second)
 

time: 303 us -> 376 us (1.24)
  blocking collectives: 39.4 us -> 182 us
  waiting for transfers between devices: 226 us -> 157 us
    all_to_all x0 -> x1, blocking collectives: none -> 142 us  [gather_over(): return jnp.concatenate(lax.all_to_all(repeated, axis, 0, 0), axis=dim)]
    all_gather x1 -> x0, waiting for transfers between devices: 68.7 us -> none  [on_device(): lax.all_gather(delta_bf, 'dp', axis=0, tiled=True).astype(jnp.float32)]
  transfers between devices with their start and end apart: 2 -> 1, of which waited for: 2 -> 1; matrix products, arithmetic and copies ran while one was open for 0% -> 0% of each run, Pallas kernels for 0% -> 0%
where the time goes in v1:
time: 376 us; the launch traced here: 375 us
  blocking collectives  182 us (48%)
  waiting for transfers between devices  157 us (42%)
  other arithmetic  20.3 us (5%)
  between operations  14 us (4%)
    reduce_scatter x1, waiting for transfers between devices, on_device(): lax.psum_scatter(local_grad.astype(jnp.float32), 'dp', scatter_dimension=...  157 us
    all_to_all x1, blocking collectives, gather_over(): return jnp.concatenate(lax.all_to_all(repeated, axis, 0, 0), axis=dim)  142 us
    psum x1, blocking collectives, on_device(): weight_sq, update_sq = lax.psum((weight_rows, update_rows), ('dp', 'mp'))  39.4 us
    convert_element_type x1, other arithmetic, on_device(): local_grad.astype(jnp.float32)  9 us
    convert_element_type x1, other arithmetic, on_device(): new_weights = (weights.astype(jnp.float32) + gather_over(delta_bf, 'dp',...  8.14 us
  transfers between devices with their start and end apart: 1, of which 1 were waited for; matrix products, arithmetic and copies ran while one was open for 0% of the time, Pallas kernels for 0%

profile of v1, /device:TPU:0, one launch (start us, length us, event | category | flops | bytes accessed | tf_op | source)
XLA Modules:
  0.0 375.2 jit_solution(5715704195342332693)
XLA Ops:
  7.2 0.0 reduce-scatter.2.cloned.1.call-start
  7.2 9.0 %bitcast_convert_fusion = f32[512,6144]{1,0:T(8,128)} fusion(bf16[1,512,6144]{2,1,0:T(8,128)(2,1)} %param.6), kind=kLoop, calls=%fused_computation.2 | loop fusion | flops 3145728 | bytes 18874368 | tf_op jit(solution)/shard_map/convert_element_type | solution.py:32
  16.2 0.0 copy-start
  16.2 0.0 copy-start.1
  16.2 0.0 copy-start.2
  16.2 0.0 reduce-scatter.2.cloned.1.call-update
  16.2 0.8 dynamic_slice.3
  17.1 156.9 %reduce-scatter.2.cloned.1.call-done = f32[16,6144]{1,0:T(8,128)} async-done(((f32[512,6144]{1,0:T(8,128)}), f32[16,6144]{1,0:T(8,128)}) %reduce-scatter.2.cloned.1.call-update) | async-done | bytes 393232 | tf_op jit(solution)/shard_map/reduce_scatter | solution.py:32
  174.0 0.0 copy-done
  174.0 0.0 copy-done.1
  174.0 0.0 copy-done.2
  174.0 2.3 multiply_reduce_fusion
  176.3 0.2 convolution_bitcast_fusion.1
  176.5 0.2 convolution_bitcast_fusion.2
  176.7 39.4 %all-reduce = (f32[16]{0:T(128)S(1)}, f32[16]{0:T(128)S(1)}) all-reduce(f32[16]{0:T(128)S(1)} %convolution_bitcast_fusion.2, f32[16]{0:T(128)S(1)} %convolution_bitcast_fusion.1), channel_id=1, replica_groups=mesh['dp'=32,'mp'=1] {'dp','mp'}, use_global_device_ids=true, to_apply=%region_1.0 | all-reduce | flops 32 | bytes 256 | tf_op jit(solution)/shard_map/psum | solution.py:43
  216.1 0.2 fusion.1
  216.2 0.9 multiply_subtract_fusion
  217.1 0.7 stack.2
  217.9 142.4 %all_to_all.5 = bf16[32,16,6144]{2,1,0:T(8,128)(2,1)S(1)} all-to-all(bf16[32,16,6144]{2,1,0:T(8,128)(2,1)S(1)} %stack.2), channel_id=1, replica_groups=mesh['dp'=32,'mp'=1] {'dp'}, dimensions={0} | all-to-all | bytes 12582912 | tf_op jit(solution)/shard_map/all_to_all | solution.py:16
  360.2 8.1 %fusion = bf16[512,6144]{1,0:T(8,128)(2,1)} fusion(bf16[512,6144]{1,0:T(8,128)(2,1)} %param.7, bf16[32,16,6144]{2,1,0:T(8,128)(2,1)S(1)} %all_to_all.5), kind=kLoop, calls=%fused_computation.1 | loop fusion | flops 12582912 | bytes 18874368 | tf_op jit(solution)/shard_map/convert_element_type | solution.py:51
Async XLA Ops:
  7.2 166.8 %reduce-scatter.2.cloned.1.call-start = ((), (), s32[]{:S(2)}) async-start(), calls=%async_computation.2 | async-start | bytes 12976128 | tf_op jit(solution)/shard_map/reduce_scatter | solution.py:32
  16.2 157.8 %copy-start = (f32[16,6144]{1,0:T(8,128)S(1)}, f32[16,6144]{1,0:T(8,128)}, u32[]{:S(2)}) copy-start(f32[16,6144]{1,0:T(8,128)} %param.8) | copy-start | bytes 1179652
  16.2 157.8 %copy-start.1 = (f32[16,6144]{1,0:T(8,128)S(1)}, f32[16,6144]{1,0:T(8,128)}, u32[]{:S(2)}) copy-start(f32[16,6144]{1,0:T(8,128)} %param.9) | copy-start | bytes 1179652
  16.2 157.8 %copy-start.2 = (f32[16,6144]{1,0:T(8,128)S(1)}, f32[16,6144]{1,0:T(8,128)}, u32[]{:S(2)}) copy-start(f32[16,6144]{1,0:T(8,128)} %param.10) | copy-start | bytes 1179652
Sparse Core Ops, SparseCore 0:
  16.4 157.5 reduce-scatter.1
